TPU v7x, 16 devices: a whole 2x2x2 slice. The times are simulated.
16 devices in a mesh: ep: 16 (over z, y, x, core).
Axes of the slice: x: 2, y: 2, z: 2, core: 2. Of those that a mesh axis runs over, the one named last changes fastest.
Arguments:
- x: bfloat16 [4096, 2048], P('ep')
- gate_w: bfloat16 [2048, 64], replicated
- up_w: bfloat16 [64, 2048, 1408], P('ep')
- down_w: bfloat16 [64, 1408, 2048], P('ep')
- expert_picks: int32 [64, 128], P('ep')
- loss_w: bfloat16 [4096, 2048], P('ep')
Outputs:
- output 1: bfloat16 [4096, 2048], P('ep')
- output 2: float32 [], replicated
- output 3: bfloat16 [4096, 2048], P('ep')
- output 4: bfloat16 [64, 2048, 1408], P('ep')
- output 5: bfloat16 [64, 1408, 2048], P('ep')
- output 6: float32 [2048, 64], replicated
All inputs are finite; a program needn't handle non-finite values.
Results may differ from a plain program's by a relative error of at most 0.02.
Values are sent between devices in bfloat16 or wider.
A program may use at most 1 GiB of HBM per device.

v0:
```python
import functools
import math
import jax
import jax.numpy as jnp
from jax import lax
from jax.experimental import pallas as pl
from jax.experimental.pallas import tpu as pltpu
from jax.sharding import PartitionSpec as P

BF = jnp.bfloat16
F32 = jnp.float32
MESH = pl.DeviceIdType.MESH
N = 16
TOK = 256
LE = 4
CAP = 128
HID = 2048
FF = 1408
CH = 512
NCH = HID // CH
ORDER = (14, 15, 6, 10, 12, 7, 11, 13, 2, 4, 8, 3, 5, 9, 1)


def dot(a, b, ca=1, cb=0):
    return lax.dot_general(a, b, (((ca,), (cb,)), ((), ())), preferred_element_type=F32)


def iota(shape, dim):
    return lax.broadcasted_iota(jnp.int32, shape, dim)


def ones_where(cond):
    return jnp.where(cond, 1.0, 0.0).astype(BF)


def split3(v):
    hi = v.astype(BF)
    rest = v - hi.astype(F32)
    mid = rest.astype(BF)
    low = (rest - mid.astype(F32)).astype(BF)
    return hi, mid, low


def flip(me, k):
    out = 0
    for b in range(4):
        bit = (me // (1 << b)) % 2
        if (k >> b) & 1:
            bit = 1 - bit
        out = out + bit * (1 << b)
    return out


def comm_kernel(scale, sel_ref, x_hbm, gw_hbm, up_hbm, dn_hbm, r_hbm,
                y_out, gx_out, gg_out, loss_out, xl_out, u_out, dh_out, da_out,
                x_v, r_v, gw_v, w1, w2, xsend, rsend, xrecv, rrecv, hsend, hrecv, gsend, grecv,
                xl_v, dh_v, u_v, gp_v, da_v, ggsend, ggrecv, ggall, selsend, selall, gates, gates_all,
                losssend, lossall, one_v, c_v, e_v, probs_v, dlog_v,
                ld_sem, w_sem, out_sem, send_sem, recv_sem):
    me = lax.axis_index('ep')
    peers = [flip(me, k) for k in ORDER]

    def load(src, dst, i):
        return pltpu.make_async_copy(src, dst, ld_sem.at[i])

    def weight1(e, slot):
        return pltpu.make_async_copy(up_hbm.at[e], w1.at[slot], w_sem.at[0, slot])

    def weight2(e, slot):
        return pltpu.make_async_copy(dn_hbm.at[e], w2.at[slot], w_sem.at[1, slot])

    def push(src, dst, peer, i):
        return pltpu.make_async_remote_copy(src_ref=src, dst_ref=dst, send_sem=send_sem.at[i], recv_sem=recv_sem.at[i],
                                            device_id=(peer,), device_id_type=MESH)

    def wait_recv(buf, i):
        part = buf.at[pl.ds(0, N - 1)]
        pltpu.make_async_copy(part, part, recv_sem.at[i]).wait()

    def wait_send(buf, i):
        part = buf.at[pl.ds(0, N - 1)]
        pltpu.make_async_copy(part, part, send_sem.at[i]).wait()

    cp_x = load(x_hbm, x_v, 0)
    cp_g = load(gw_hbm, gw_v, 1)
    cp_r = load(r_hbm, r_v, 2)
    cp_x.start()
    cp_g.start()
    cp_r.start()

    sel = sel_ref[...]
    selsend[...] = jnp.zeros_like(selsend)
    selsend[0:LE, :] = sel
    selall[pl.ds(me, 1)] = selsend[...].reshape(1, 8, CAP)

    barrier = pltpu.get_barrier_semaphore()
    for p in peers:
        pl.semaphore_signal(barrier, inc=1, device_id=(p,), device_id_type=MESH)
    pl.semaphore_wait(barrier, N - 1)

    for p in peers:
        push(selsend, selall.at[me], p, 0).start()
    for e in range(3):
        weight1(e, e).start()
        weight2(e, e).start()

    cp_g.wait()
    cp_x.wait()
    logits = dot(x_v[...], gw_v[...], 1, 1)
    ex = jnp.exp(logits - jnp.max(logits, axis=1, keepdims=True))
    probs = ex / jnp.sum(ex, axis=1, keepdims=True)
    probs_v[...] = probs

    below = ones_where(iota((TOK, TOK), 1) < iota((TOK, TOK), 0))
    slot_lane = (iota((TOK, TOK), 1) % 16).astype(F32)

    tok_row = iota((TOK, CAP), 0)
    same = iota((CAP, TOK), 0) // 8 == iota((CAP, TOK), 1) // 16
    fold = ones_where(same)
    base = (iota((1, CAP), 1) // 8) * TOK
    hits = [ones_where(tok_row == sel[l:l + 1, :] - base) for l in range(LE)]
    count = dot(hits[0], fold)
    for l in range(1, LE):
        count = count + dot(hits[l], fold)
    pres = count > 0.5
    rank = dot(below, ones_where(pres))
    pick_of = jnp.where(pres, jnp.where(rank == slot_lane, 1.0, 0.0), 0.0).astype(BF)
    for l in range(LE):
        e_v[l] = jnp.where(same, dot(hits[l], pick_of, 0, 0), 0.0).astype(BF)

    for_wait = selall.at[pl.ds(0, N - 1)]
    pltpu.make_async_copy(for_wait, for_wait, recv_sem.at[0]).wait()
    everyone = selall[...].reshape(8 * N, CAP)
    mine = jnp.where(iota((8 * N, CAP), 1) // 8 == me, everyone - me * TOK, 0).astype(F32).astype(BF)
    place = ones_where(iota((CAP, 512), 0) % 8 == iota((CAP, 512), 1) % 8)
    spread = dot(mine, place)
    lane = iota((8 * N, 512), 1)
    want = ((lane % 256) // 16) * 8 + 2 * (lane // 256) + (lane % 16) // 8
    ids = jnp.sum(jnp.where(iota((8 * N, 512), 0) == want, spread, 0.0), axis=0, keepdims=True)
    one = jnp.where(iota((TOK, 512), 0).astype(F32) == ids, 1.0, 0.0)
    one_v[...] = one.astype(BF)
    fold2 = ones_where((iota((512, TOK), 0) % 256) // 16 == iota((512, TOK), 1) // 16)
    pres2 = dot(one_v[...], fold2) > 0.5
    rank2 = dot(below, ones_where(pres2))
    give = jnp.where(pres2, jnp.where(rank2 == slot_lane, 1.0, 0.0), 0.0).astype(BF)
    give_t = give.T

    def gather(src, dst):
        def step(c, carry):
            cols = pl.ds(pl.multiple_of(c * CH, CH), CH)
            dst[:, :, cols] = dot(give_t, src[:, cols]).astype(BF).reshape(N, 16, CH)
            return carry
        lax.fori_loop(0, NCH, step, 0)

    gather(x_v, xsend)
    for p in peers:
        push(xsend.at[p], xrecv.at[me], p, 1).start()
    xrecv[pl.ds(me, 1)] = xsend[pl.ds(me, 1)]

    rep = ones_where(iota((64, 512), 0) == 4 * ((iota((64, 512), 1) % 256) // 16) + 2 * (iota((64, 512), 1) // 256)
                     + (iota((64, 512), 1) % 16) // 8)
    wide = 0.0
    for term in split3(probs_v[...]):
        wide = wide + dot(term, rep)
    comb = wide * one
    for i, term in enumerate(split3(comb)):
        c_v[i] = term
    gates[...] = jnp.sum(comb, axis=0, keepdims=True)
    for p in peers:
        push(gates, gates_all.at[me], p, 2).start()
    gates_all[pl.ds(me, 1)] = gates[...].reshape(1, 1, 512)

    cp_r.wait()
    gather(r_v, rsend)
    for p in peers:
        push(rsend.at[p], rrecv.at[me], p, 3).start()
    rrecv[pl.ds(me, 1)] = rsend[pl.ds(me, 1)]

    wait_recv(xrecv, 1)

    def fwd(q, carry):
        for j in range(2):
            e = 2 * q + j
            slot = e % 3
            xl = dot(e_v[e], xrecv[...].reshape(TOK, HID)).astype(BF)
            xl_v[e] = xl
            weight1(e, slot).wait()
            a = dot(xl_v[e], w1[slot])
            if j == 0:
                @pl.when(q == 0)
                def _():
                    weight1(3, 0).start()
            k0 = math.sqrt(2.0 / math.pi)
            t = jnp.tanh(k0 * (a + 0.044715 * (a * a * a)))
            u_v[e] = (0.5 * a * (1.0 + t)).astype(BF)
            gp_v[e] = 0.5 * (1.0 + t) + 0.5 * a * (1.0 - t * t) * (k0 * (1.0 + 3.0 * 0.044715 * (a * a)))
        weight2(2 * q, (2 * q) % 3).wait()
        weight2(2 * q + 1, (2 * q + 1) % 3).wait()

        def step(c, carry):
            cols = pl.ds(pl.multiple_of(c * CH, CH), CH)
            outs = [dot(u_v[2 * q + j], w2[(2 * q + j) % 3, :, cols]).reshape(N, 8, CH) for j in range(2)]
            hsend[q, :, :, cols] = jnp.concatenate(outs, axis=1).astype(BF)
            return carry
        lax.fori_loop(0, NCH, step, 0)

        @pl.when(q == 0)
        def _():
            weight2(3, 0).start()
        for p in peers:
            push(hsend.at[q, p], hrecv.at[q, me], p, 4 + q).start()
        hrecv[q, pl.ds(me, 1)] = hsend[q, pl.ds(me, 1)]
        return carry
    lax.fori_loop(0, 2, fwd, 0)
    pltpu.make_async_copy(xl_v, xl_out, out_sem.at[0]).start()
    pltpu.make_async_copy(u_v, u_out, out_sem.at[1]).start()

    wait_recv(gates_all, 2)
    wait_recv(rrecv, 3)

    def bwd(q, carry):
        for j in range(2):
            e = 2 * (1 - q) + j
            slot = (1 - q) * (2 - 2 * j) + q * (2 - j)
            if j == 0:
                @pl.when(q == 1)
                def _():
                    weight1(0, 2).wait()
                    weight2(0, 2).wait()
            rows = jnp.broadcast_to(gates_all[...], (N, 8, 512)).reshape(CAP, 512)
            here = iota((CAP, 512), 1) == (1 - q) * 256 + me * 16 + j * 8 + iota((CAP, 512), 0) % 8
            gcol = jnp.sum(jnp.where(here, rows, 0.0), axis=1, keepdims=True)

            def rstep(c, carry):
                cols = pl.ds(pl.multiple_of(c * CH, CH), CH)
                rl = dot(e_v[e], rrecv[:, :, cols].reshape(TOK, CH))
                dh_v[e, :, cols] = (gcol * (rl * scale)).astype(BF)
                return carry
            lax.fori_loop(0, NCH, rstep, 0)
            du = dot(dh_v[e], w2[slot], 1, 1).astype(BF).astype(F32)
            if j == 0:
                @pl.when(q == 0)
                def _():
                    weight2(0, 2).start()
            da_v[e] = (gp_v[e] * du).astype(BF)

        def step(c, carry):
            cols = pl.ds(pl.multiple_of(c * CH, CH), CH)
            outs = []
            for j in range(2):
                slot = (1 - q) * (2 - 2 * j) + q * (2 - j)
                outs.append(dot(da_v[2 * (1 - q) + j], w1[slot, cols, :], 1, 1).reshape(N, 8, CH))
            gsend[1 - q, :, :, cols] = jnp.concatenate(outs, axis=1).astype(BF)
            return carry
        lax.fori_loop(0, NCH, step, 0)

        @pl.when(q == 0)
        def _():
            weight1(0, 2).start()
        for p in peers:
            push(gsend.at[1 - q, p], grecv.at[1 - q, me], p, 6 + q).start()
        grecv[1 - q, pl.ds(me, 1)] = gsend[1 - q, pl.ds(me, 1)]
        return carry
    lax.fori_loop(0, 2, bwd, 0)
    pltpu.make_async_copy(dh_v, dh_out, out_sem.at[2]).start()
    pltpu.make_async_copy(da_v, da_out, out_sem.at[3]).start()

    wait_recv(hrecv.at[0], 4)
    wait_recv(hrecv.at[1], 5)
    inner = dot(r_v[...], hrecv[...].reshape(512, HID), 1, 1)
    masked = inner * one_v[...].astype(F32)
    gather_e = ones_where(iota((512, 64), 1) == 4 * ((iota((512, 64), 0) % 256) // 16) + 2 * (iota((512, 64), 0) // 256)
                          + (iota((512, 64), 0) % 16) // 8)
    ds = 0.0
    for term in split3(masked):
        ds = ds + dot(term, gather_e)
    ds = ds * scale
    probs = probs_v[...]
    dlog = (probs * (ds - jnp.sum(probs * ds, axis=1, keepdims=True))).astype(BF)
    dlog_v[...] = dlog
    dlog_t = dlog.astype(F32).T.astype(BF)
    for c in range(NCH):
        part = dot(dlog_t, x_v[:, c * CH:(c + 1) * CH])
        for i in range(CH // 128):
            ggsend[c * (CH // 128) + i] = part[:, i * 128:(i + 1) * 128]
    for p in peers:
        push(ggsend.at[p], ggrecv.at[me], p, 8).start()
    ggrecv[pl.ds(me, 1)] = ggsend[pl.ds(me, 1)]

    wait_send(xsend, 1)

    def ystep(c, acc):
        cols = pl.ds(pl.multiple_of(c * CH, CH), CH)
        h = hrecv[:, :, :, cols].reshape(512, CH)
        tot = x_v[:, cols].astype(F32) + (dot(c_v[0], h) + dot(c_v[1], h) + dot(c_v[2], h))
        y = tot.astype(BF)
        xsend[:, :, cols] = y.reshape(N, 16, CH)
        return acc + jnp.sum(y.astype(F32) * r_v[:, cols].astype(F32), axis=0, keepdims=True)
    losssend[...] = lax.fori_loop(0, NCH, ystep, jnp.zeros((1, CH), F32))
    cp_y = pltpu.make_async_copy(xsend, y_out, out_sem.at[4])
    cp_y.start()
    for p in peers:
        push(losssend, lossall.at[me], p, 9).start()
    lossall[pl.ds(me, 1)] = losssend[...].reshape(1, 1, CH)

    wait_recv(ggrecv, 8)
    total = ggrecv[0]
    for i in range(1, N):
        total = total + ggrecv[i]
    wait_send(ggsend, 8)
    ggsend[0] = total
    for p in peers:
        push(ggsend.at[0], ggall.at[me], p, 10).start()
    ggall[pl.ds(me, 1)] = total.reshape(1, 64, 128)

    wait_send(rsend, 3)
    wait_recv(grecv.at[1], 6)
    wait_recv(grecv.at[0], 7)

    def gstep(c, carry):
        cols = pl.ds(pl.multiple_of(c * CH, CH), CH)
        tot = r_v[:, cols].astype(F32) * scale + dot(one_v[...], grecv[:, :, :, cols].reshape(512, CH))
        tot = tot + dot(dlog_v[...], gw_v[:, cols])
        rsend[:, :, cols] = tot.astype(BF).reshape(N, 16, CH)
        return carry
    lax.fori_loop(0, NCH, gstep, 0)
    cp_gx = pltpu.make_async_copy(rsend, gx_out, out_sem.at[5])
    cp_gx.start()

    wait_recv(lossall, 9)
    loss_out[0, 0] = jnp.sum(lossall[...]) * scale
    wait_recv(ggall, 10)
    cp_gg = [pltpu.make_async_copy(ggall.at[i], gg_out.at[:, pl.ds(i * 128, 128)], out_sem.at[6]) for i in range(N)]
    for cp in cp_gg:
        cp.start()

    wait_send(selall, 0)
    wait_send(gates_all, 2)
    wait_send(hsend.at[0], 4)
    wait_send(hsend.at[1], 5)
    wait_send(gsend.at[1], 6)
    wait_send(gsend.at[0], 7)
    wait_send(lossall, 9)
    wait_send(ggall, 10)
    pltpu.make_async_copy(xl_v, xl_out, out_sem.at[0]).wait()
    pltpu.make_async_copy(u_v, u_out, out_sem.at[1]).wait()
    pltpu.make_async_copy(dh_v, dh_out, out_sem.at[2]).wait()
    pltpu.make_async_copy(da_v, da_out, out_sem.at[3]).wait()
    cp_y.wait()
    cp_gx.wait()
    for cp in cp_gg:
        cp.wait()


def comm_call(sel, x, gw, up, dn, r, scale):
    any_ = pl.BlockSpec(memory_space=pl.ANY)
    vmem = pl.BlockSpec(memory_space=pltpu.VMEM)
    V = pltpu.VMEM
    shape = jax.ShapeDtypeStruct
    return pl.pallas_call(
        functools.partial(comm_kernel, scale),
        out_shape=[shape((N, 16, HID), BF), shape((N, 16, HID), BF), shape((64, HID), F32), shape((1, 1), F32),
                   shape((LE, CAP, HID), BF), shape((LE, CAP, FF), BF), shape((LE, CAP, HID), BF), shape((LE, CAP, FF), BF)],
        in_specs=[vmem, any_, any_, any_, any_, any_],
        out_specs=[any_, any_, any_, pl.BlockSpec(memory_space=pltpu.SMEM), any_, any_, any_, any_],
        scratch_shapes=[
            V((TOK, HID), BF), V((TOK, HID), BF), V((64, HID), BF),
            V((3, HID, FF), BF), V((3, FF, HID), BF),
            V((N, 16, HID), BF), V((N, 16, HID), BF), V((N, 16, HID), BF), V((N, 16, HID), BF),
            V((2, N, 16, HID), BF), V((2, N, 16, HID), BF), V((2, N, 16, HID), BF), V((2, N, 16, HID), BF),
            V((LE, CAP, HID), BF), V((LE, CAP, HID), BF), V((LE, CAP, FF), BF), V((LE, CAP, FF), F32), V((LE, CAP, FF), BF),
            V((N, 64, 128), F32), V((N, 64, 128), F32), V((N, 64, 128), F32),
            V((8, CAP), jnp.int32), V((N, 8, CAP), jnp.int32), V((1, 512), F32), V((N, 1, 512), F32),
            V((1, CH), F32), V((N, 1, CH), F32),
            V((TOK, 512), BF), V((3, TOK, 512), BF), V((LE, CAP, TOK), BF), V((TOK, 64), F32), V((TOK, 64), BF),
            pltpu.SemaphoreType.DMA((3,)), pltpu.SemaphoreType.DMA((2, 3)), pltpu.SemaphoreType.DMA((7,)),
            pltpu.SemaphoreType.DMA((11,)), pltpu.SemaphoreType.DMA((11,)),
        ],
        compiler_params=pltpu.CompilerParams(collective_id=0, has_side_effects=True, vmem_limit_bytes=67043328),
        name='exchange',
    )(sel, x, gw, up, dn, r)


def wgrad_kernel(xl, da, u, dh, y_in, gx_in, gg_in, loss_in, g1, g2, y, gx, gg, loss):
    g1[0] = dot(xl[0], da[0], 0, 0).astype(BF)
    g2[0] = dot(u[0], dh[0], 0, 0).astype(BF)
    y[...] = y_in[...]
    gx[...] = gx_in[...]
    gg[...] = gg_in[...]

    @pl.when((pl.program_id(0) == 0) & (pl.program_id(1) == 0))
    def _():
        loss[0, 0] = loss_in[0, 0]


def wgrad_call(xl, u, dh, da, y, gx, gg, loss):
    shape = jax.ShapeDtypeStruct
    rows = pl.BlockSpec((1, 16, HID), lambda e, c: (e * NCH + c, 0, 0))
    cols = pl.BlockSpec((64, 128), lambda e, c: (0, e * NCH + c))
    whole = pl.BlockSpec(memory_space=pltpu.SMEM)
    return pl.pallas_call(
        wgrad_kernel,
        grid=(LE, NCH),
        in_specs=[pl.BlockSpec((1, CAP, CH), lambda e, c: (e, 0, c)), pl.BlockSpec((1, CAP, FF), lambda e, c: (e, 0, 0)),
                  pl.BlockSpec((1, CAP, FF), lambda e, c: (e, 0, 0)), pl.BlockSpec((1, CAP, CH), lambda e, c: (e, 0, c)),
                  rows, rows, cols, whole],
        out_specs=[pl.BlockSpec((1, CH, FF), lambda e, c: (e, c, 0)), pl.BlockSpec((1, FF, CH), lambda e, c: (e, 0, c)),
                   rows, rows, cols, whole],
        out_shape=[shape((LE, HID, FF), BF), shape((LE, FF, HID), BF), shape((N, 16, HID), BF), shape((N, 16, HID), BF),
                   shape((64, HID), F32), shape((1, 1), F32)],
        compiler_params=pltpu.CompilerParams(vmem_limit_bytes=67043328),
        name='weight_grads',
    )(xl, da, u, dh, y, gx, gg, loss)


def solution(mesh):
    def device_step(x, gate_w, up_w, down_w, expert_picks, loss_w):
        scale = 1.0 / math.sqrt(TOK * N * HID)
        y, gx, gg, loss, xl, u, dh, da = comm_call(expert_picks, x, gate_w.T, up_w, down_w, loss_w, scale)
        grad_up, grad_down, y, gx, gg, loss = wgrad_call(xl, u, dh, da, y, gx, gg, loss)
        return y.reshape(TOK, HID), loss[0, 0], gx.reshape(TOK, HID), grad_up, grad_down, gg.T

    return jax.shard_map(device_step, mesh=mesh,
                         in_specs=(P('ep'), P(), P('ep'), P('ep'), P('ep'), P('ep')),
                         out_specs=(P('ep'), P(), P('ep'), P('ep'), P('ep'), P()),
                         check_vma=False)
```

profile of v0, /device:TPU:0, one launch (start us, length us, event | category | flops | bytes accessed | tf_op | source)
XLA Modules:
  0.0 123.0 jit_solution(8728793693088627139)
XLA Ops:
  0.6 97.8 %exchange.1 = (bf16[16,16,2048]{2,1,0:T(8,128)(2,1)}, bf16[16,16,2048]{2,1,0:T(8,128)(2,1)}, f32[64,2048]{1,0:T(8,128)}, f32[1,1]{1,0:T(1,128)}, bf16[4,128,2048...) custom-call(s32[4,128]{1,0:T(4,128)} %sel_ref.1, ...), custom_call_target="tpu_custom_call" | custom-call | tf_op jit(solution)/shard_map/exchange/pallas_call | solution.py:360
  98.4 24.6 %weight_grads.1 = (bf16[4,2048,1408]{2,1,0:T(8,128)(2,1)}, bf16[4,1408,2048]{2,1,0:T(8,128)(2,1)}, bf16[16,16,2048]{2,1,0:T(8,128)(2,1)}, bf16[16,16,2048]{2,1,0...) custom-call(bf16[4,128,2048]{2,1,0:T(8,128)(2,1)} %get-tuple-element.20.xl, ...), custom_call_target="tpu_custom_call" | custom-call | tf_op jit(solution)/shard_map/weight_grads/pallas_call | solution.py:401
where the time goes:
time: 124 us; the launch traced here: 123 us
  Pallas kernels  122 us (98%)
    pallas_call x1, Pallas kernels, comm_call(): pl.pallas_call(functools.partial(comm_kernel, scale), out_shape=[shape((N...  97.8 us
    pallas_call x1, Pallas kernels, wgrad_call(): pl.pallas_call(wgrad_kernel, grid=(LE, NCH), in_specs=[pl.BlockSpec((1, C...  24.6 us

commit v1 on v0

--- a/solution.py
+++ b/solution.py
@@ -18,6 +18,7 @@
 FF = 1408
 CH = 512
 NCH = HID // CH
+NOW = 2
 ORDER = (14, 15, 6, 10, 12, 7, 11, 13, 2, 4, 8, 3, 5, 9, 1)
 
 
@@ -52,13 +53,15 @@
 
 
 def comm_kernel(scale, sel_ref, x_hbm, gw_hbm, up_hbm, dn_hbm, r_hbm,
-                y_out, gx_out, gg_out, loss_out, xl_out, u_out, dh_out, da_out,
-                x_v, r_v, gw_v, w1, w2, xsend, rsend, xrecv, rrecv, hsend, hrecv, gsend, grecv,
-                xl_v, dh_v, u_v, gp_v, da_v, ggsend, ggrecv, ggall, selsend, selall, gates, gates_all,
+                y_out, gnow_out, glater_out, one_out, dlog_out, gg_out, loss_out, xl_out, u_out, dh_out, da_out,
+                x_v, r_v, gw_v, w1, w2, xsend, rsend, xrecv, rrecv, hsend, hrecv, gsend,
+                xl_v, dh_v, u_v, gp_v, da_v, ggpart, ggpair, gghalf, ggrecv, ggall, selsend, selall, gates, gates_all,
                 losssend, lossall, one_v, c_v, e_v, probs_v, dlog_v,
                 ld_sem, w_sem, out_sem, send_sem, recv_sem):
     me = lax.axis_index('ep')
     peers = [flip(me, k) for k in ORDER]
+    core, chip, twin = me % 2, me // 2, flip(me, 1)
+    others = [flip(me, k) for k in ORDER if k % 2 == 0]
 
     def load(src, dst, i):
         return pltpu.make_async_copy(src, dst, ld_sem.at[i])
@@ -73,12 +76,12 @@
         return pltpu.make_async_remote_copy(src_ref=src, dst_ref=dst, send_sem=send_sem.at[i], recv_sem=recv_sem.at[i],
                                             device_id=(peer,), device_id_type=MESH)
 
-    def wait_recv(buf, i):
-        part = buf.at[pl.ds(0, N - 1)]
+    def wait_recv(buf, i, n=N - 1):
+        part = buf.at[pl.ds(0, n)]
         pltpu.make_async_copy(part, part, recv_sem.at[i]).wait()
 
-    def wait_send(buf, i):
-        part = buf.at[pl.ds(0, N - 1)]
+    def wait_send(buf, i, n=N - 1):
+        part = buf.at[pl.ds(0, n)]
         pltpu.make_async_copy(part, part, send_sem.at[i]).wait()
 
     cp_x = load(x_hbm, x_v, 0)
@@ -218,6 +221,12 @@
     wait_recv(gates_all, 2)
     wait_recv(rrecv, 3)
 
+    def send_now(c):
+        cols = pl.ds(c * CH, CH)
+        for p in peers:
+            push(gsend.at[1, p, :, cols], gnow_out.at[me, :, cols], p, 6 + c).start()
+        pltpu.make_async_copy(gsend.at[1, me, :, cols], gnow_out.at[me, :, cols], out_sem.at[7 + c]).start()
+
     def bwd(q, carry):
         for j in range(2):
             e = 2 * (1 - q) + j
@@ -257,11 +266,16 @@
         @pl.when(q == 0)
         def _():
             weight1(0, 2).start()
-        for p in peers:
-            push(gsend.at[1 - q, p], grecv.at[1 - q, me], p, 6 + q).start()
-        grecv[1 - q, pl.ds(me, 1)] = gsend[1 - q, pl.ds(me, 1)]
+        @pl.when(q == 0)
+        def _():
+            send_now(0)
         return carry
     lax.fori_loop(0, 2, bwd, 0)
+    later = [pltpu.make_async_copy(gsend.at[0], glater_out.at[:, :, pl.ds(0, HID)], out_sem.at[5]),
+             pltpu.make_async_copy(gsend.at[1, :, :, pl.ds(NOW * CH, HID - NOW * CH)],
+                                   glater_out.at[:, :, pl.ds(HID, HID - NOW * CH)], out_sem.at[9])]
+    for cp in later:
+        cp.start()
     pltpu.make_async_copy(dh_v, dh_out, out_sem.at[2]).start()
     pltpu.make_async_copy(da_v, da_out, out_sem.at[3]).start()
 
@@ -282,10 +296,18 @@
     for c in range(NCH):
         part = dot(dlog_t, x_v[:, c * CH:(c + 1) * CH])
         for i in range(CH // 128):
-            ggsend[c * (CH // 128) + i] = part[:, i * 128:(i + 1) * 128]
-    for p in peers:
-        push(ggsend.at[p], ggrecv.at[me], p, 8).start()
-    ggrecv[pl.ds(me, 1)] = ggsend[pl.ds(me, 1)]
+            ggpart[c // 2, (c % 2) * (CH // 128) + i] = part[:, i * 128:(i + 1) * 128]
+    push(ggpart.at[1 - core], ggpair, twin, 8).start()
+    cp_dlog = pltpu.make_async_copy(dlog_v, dlog_out, out_sem.at[10])
+    cp_dlog.start()
+    cp_one = pltpu.make_async_copy(one_v, one_out, out_sem.at[11])
+    cp_one.start()
+    push(ggpart.at[1 - core], ggpair, twin, 8).wait_recv()
+    gghalf[...] = ggpart[core] + ggpair[...]
+    for p in others:
+        push(gghalf.at[p // 2], ggrecv.at[chip], p, 10).start()
+    ggrecv[pl.ds(chip, 1)] = gghalf[pl.ds(chip, 1)]
+    send_now(1)
 
     wait_send(xsend, 1)
 
@@ -303,51 +325,51 @@
         push(losssend, lossall.at[me], p, 9).start()
     lossall[pl.ds(me, 1)] = losssend[...].reshape(1, 1, CH)
 
-    wait_recv(ggrecv, 8)
+    wait_recv(ggrecv, 10, 7)
     total = ggrecv[0]
-    for i in range(1, N):
+    for i in range(1, 8):
         total = total + ggrecv[i]
-    wait_send(ggsend, 8)
-    ggsend[0] = total
-    for p in peers:
-        push(ggsend.at[0], ggall.at[me], p, 10).start()
-    ggall[pl.ds(me, 1)] = total.reshape(1, 64, 128)
-
-    wait_send(rsend, 3)
-    wait_recv(grecv.at[1], 6)
-    wait_recv(grecv.at[0], 7)
-
-    def gstep(c, carry):
-        cols = pl.ds(pl.multiple_of(c * CH, CH), CH)
-        tot = r_v[:, cols].astype(F32) * scale + dot(one_v[...], grecv[:, :, :, cols].reshape(512, CH))
-        tot = tot + dot(dlog_v[...], gw_v[:, cols])
-        rsend[:, :, cols] = tot.astype(BF).reshape(N, 16, CH)
-        return carry
-    lax.fori_loop(0, NCH, gstep, 0)
-    cp_gx = pltpu.make_async_copy(rsend, gx_out, out_sem.at[5])
-    cp_gx.start()
-
+    ggall[core, pl.ds(chip, 1)] = total.reshape(1, 64, 128)
+    for p in others:
+        push(ggall.at[core, chip], ggall.at[core, chip], p, 11).start()
     wait_recv(lossall, 9)
     loss_out[0, 0] = jnp.sum(lossall[...]) * scale
-    wait_recv(ggall, 10)
-    cp_gg = [pltpu.make_async_copy(ggall.at[i], gg_out.at[:, pl.ds(i * 128, 128)], out_sem.at[6]) for i in range(N)]
+    wait_recv(ggall.at[core], 11, 7)
+    across = push(ggall.at[core], ggall.at[core], twin, 12)
+    across.start()
+    across.wait_recv()
+    cp_gg = [pltpu.make_async_copy(ggall.at[i // 8, i % 8], gg_out.at[:, pl.ds(i * 128, 128)], out_sem.at[6]) for i in range(N)]
     for cp in cp_gg:
         cp.start()
+    for c in range(NOW):
+        cols = pl.ds(c * CH, CH)
+        part = gnow_out.at[pl.ds(0, N - 1), :, cols]
+        pltpu.make_async_copy(part, part, recv_sem.at[6 + c]).wait()
 
     wait_send(selall, 0)
     wait_send(gates_all, 2)
     wait_send(hsend.at[0], 4)
     wait_send(hsend.at[1], 5)
-    wait_send(gsend.at[1], 6)
-    wait_send(gsend.at[0], 7)
+    for c in range(NOW):
+        cols = pl.ds(c * CH, CH)
+        part = gsend.at[1, pl.ds(0, N - 1), :, cols]
+        pltpu.make_async_copy(part, part, send_sem.at[6 + c]).wait()
+        pltpu.make_async_copy(gsend.at[1, me, :, cols], gnow_out.at[me, :, cols], out_sem.at[7 + c]).wait()
+    wait_send(rsend, 3)
     wait_send(lossall, 9)
-    wait_send(ggall, 10)
+    push(ggpart.at[1 - core], ggpair, twin, 8).wait_send()
+    wait_send(gghalf, 10, 7)
+    wait_send(ggall.at[core], 11, 7)
+    across.wait_send()
+    for cp in later:
+        cp.wait()
+    cp_dlog.wait()
+    cp_one.wait()
     pltpu.make_async_copy(xl_v, xl_out, out_sem.at[0]).wait()
     pltpu.make_async_copy(u_v, u_out, out_sem.at[1]).wait()
     pltpu.make_async_copy(dh_v, dh_out, out_sem.at[2]).wait()
     pltpu.make_async_copy(da_v, da_out, out_sem.at[3]).wait()
     cp_y.wait()
-    cp_gx.wait()
     for cp in cp_gg:
         cp.wait()
 
@@ -359,66 +381,137 @@
     shape = jax.ShapeDtypeStruct
     return pl.pallas_call(
         functools.partial(comm_kernel, scale),
-        out_shape=[shape((N, 16, HID), BF), shape((N, 16, HID), BF), shape((64, HID), F32), shape((1, 1), F32),
+        out_shape=[shape((N, 16, HID), BF), shape((N, 16, NOW * CH), BF), shape((N, 16, 2 * HID - NOW * CH), BF), shape((TOK, 512), BF),
+                   shape((TOK, 64), BF), shape((64, HID), F32), shape((1, 1), F32),
                    shape((LE, CAP, HID), BF), shape((LE, CAP, FF), BF), shape((LE, CAP, HID), BF), shape((LE, CAP, FF), BF)],
         in_specs=[vmem, any_, any_, any_, any_, any_],
-        out_specs=[any_, any_, any_, pl.BlockSpec(memory_space=pltpu.SMEM), any_, any_, any_, any_],
+        out_specs=[any_, any_, any_, any_, any_, any_, pl.BlockSpec(memory_space=pltpu.SMEM), any_, any_, any_, any_],
         scratch_shapes=[
             V((TOK, HID), BF), V((TOK, HID), BF), V((64, HID), BF),
             V((3, HID, FF), BF), V((3, FF, HID), BF),
             V((N, 16, HID), BF), V((N, 16, HID), BF), V((N, 16, HID), BF), V((N, 16, HID), BF),
-            V((2, N, 16, HID), BF), V((2, N, 16, HID), BF), V((2, N, 16, HID), BF), V((2, N, 16, HID), BF),
+            V((2, N, 16, HID), BF), V((2, N, 16, HID), BF), V((2, N, 16, HID), BF),
             V((LE, CAP, HID), BF), V((LE, CAP, HID), BF), V((LE, CAP, FF), BF), V((LE, CAP, FF), F32), V((LE, CAP, FF), BF),
-            V((N, 64, 128), F32), V((N, 64, 128), F32), V((N, 64, 128), F32),
+            V((2, 8, 64, 128), F32), V((8, 64, 128), F32), V((8, 64, 128), F32), V((8, 64, 128), F32), V((2, 8, 64, 128), F32),
             V((8, CAP), jnp.int32), V((N, 8, CAP), jnp.int32), V((1, 512), F32), V((N, 1, 512), F32),
             V((1, CH), F32), V((N, 1, CH), F32),
             V((TOK, 512), BF), V((3, TOK, 512), BF), V((LE, CAP, TOK), BF), V((TOK, 64), F32), V((TOK, 64), BF),
-            pltpu.SemaphoreType.DMA((3,)), pltpu.SemaphoreType.DMA((2, 3)), pltpu.SemaphoreType.DMA((7,)),
-            pltpu.SemaphoreType.DMA((11,)), pltpu.SemaphoreType.DMA((11,)),
+            pltpu.SemaphoreType.DMA((3,)), pltpu.SemaphoreType.DMA((2, 3)), pltpu.SemaphoreType.DMA((12,)),
+            pltpu.SemaphoreType.DMA((13,)), pltpu.SemaphoreType.DMA((13,)),
         ],
         compiler_params=pltpu.CompilerParams(collective_id=0, has_side_effects=True, vmem_limit_bytes=67043328),
         name='exchange',
     )(sel, x, gw, up, dn, r)
 
 
-def wgrad_kernel(xl, da, u, dh, y_in, gx_in, gg_in, loss_in, g1, g2, y, gx, gg, loss):
-    g1[0] = dot(xl[0], da[0], 0, 0).astype(BF)
-    g2[0] = dot(u[0], dh[0], 0, 0).astype(BF)
-    y[...] = y_in[...]
-    gx[...] = gx_in[...]
-    gg[...] = gg_in[...]
-
-    @pl.when((pl.program_id(0) == 0) & (pl.program_id(1) == 0))
-    def _():
-        loss[0, 0] = loss_in[0, 0]
-
-
-def wgrad_call(xl, u, dh, da, y, gx, gg, loss):
+def wgrad_kernel(xl_in, u_in, dh_in, da_in, y_in, gg_in, loss_in, g1, g2, y, gg, loss,
+                 xl_v, u_v, dh_v, da_v, y_v, gg_v, t1, t2, in_sem, out_sem):
+    def loads(e):
+        return [pltpu.make_async_copy(src.at[e], dst.at[e], in_sem.at[e])
+                for src, dst in ((xl_in, xl_v), (da_in, da_v), (u_in, u_v), (dh_in, dh_v))]
+
+    def stores(i):
+        e, c = i // NCH, i % NCH
+        cols = pl.ds(pl.multiple_of(c * CH, CH), CH)
+        return [pltpu.make_async_copy(t1.at[i], g1.at[e, cols, :], out_sem.at[0]),
+                pltpu.make_async_copy(t2.at[i], g2.at[e, :, cols], out_sem.at[1])]
+
+    for e in range(LE):
+        for cp in loads(e):
+            cp.start()
+    cp_y = pltpu.make_async_copy(y_in, y_v, in_sem.at[LE])
+    cp_gg = pltpu.make_async_copy(gg_in, gg_v, in_sem.at[LE + 1])
+    cp_y.start()
+    cp_gg.start()
+    loss[0, 0] = loss_in[0, 0]
+
+    def step(i, carry):
+        e, c = i // NCH, i % NCH
+
+        @pl.when(c == 0)
+        def _():
+            for cp in loads(e):
+                cp.wait()
+        cols = pl.ds(pl.multiple_of(c * CH, CH), CH)
+        t1[i] = dot(xl_v[e, :, cols], da_v[e], 0, 0).astype(BF)
+        t2[i] = dot(u_v[e], dh_v[e, :, cols], 0, 0).astype(BF)
+        for cp in stores(i):
+            cp.start()
+        return carry
+    lax.fori_loop(0, LE * NCH, step, 0)
+    cp_y.wait()
+    cp_gg.wait()
+    out_y = pltpu.make_async_copy(y_v, y, in_sem.at[LE])
+    out_gg = pltpu.make_async_copy(gg_v, gg, in_sem.at[LE + 1])
+    out_y.start()
+    out_gg.start()
+    out_y.wait()
+    out_gg.wait()
+
+    def finish(i, carry):
+        for cp in stores(i):
+            cp.wait()
+        return carry
+    lax.fori_loop(0, LE * NCH, finish, 0)
+
+
+def wgrad_call(xl, u, dh, da, y, gg, loss):
     shape = jax.ShapeDtypeStruct
-    rows = pl.BlockSpec((1, 16, HID), lambda e, c: (e * NCH + c, 0, 0))
-    cols = pl.BlockSpec((64, 128), lambda e, c: (0, e * NCH + c))
-    whole = pl.BlockSpec(memory_space=pltpu.SMEM)
+    any_ = pl.BlockSpec(memory_space=pl.ANY)
+    smem = pl.BlockSpec(memory_space=pltpu.SMEM)
+    V = pltpu.VMEM
     return pl.pallas_call(
         wgrad_kernel,
-        grid=(LE, NCH),
-        in_specs=[pl.BlockSpec((1, CAP, CH), lambda e, c: (e, 0, c)), pl.BlockSpec((1, CAP, FF), lambda e, c: (e, 0, 0)),
-                  pl.BlockSpec((1, CAP, FF), lambda e, c: (e, 0, 0)), pl.BlockSpec((1, CAP, CH), lambda e, c: (e, 0, c)),
-                  rows, rows, cols, whole],
-        out_specs=[pl.BlockSpec((1, CH, FF), lambda e, c: (e, c, 0)), pl.BlockSpec((1, FF, CH), lambda e, c: (e, 0, c)),
-                   rows, rows, cols, whole],
-        out_shape=[shape((LE, HID, FF), BF), shape((LE, FF, HID), BF), shape((N, 16, HID), BF), shape((N, 16, HID), BF),
-                   shape((64, HID), F32), shape((1, 1), F32)],
+        in_specs=[any_] * 6 + [smem],
+        out_specs=[any_] * 4 + [smem],
+        out_shape=[shape((LE, HID, FF), BF), shape((LE, FF, HID), BF), shape((N, 16, HID), BF), shape((64, HID), F32), shape((1, 1), F32)],
+        scratch_shapes=[V((LE, CAP, HID), BF), V((LE, CAP, FF), BF), V((LE, CAP, HID), BF), V((LE, CAP, FF), BF),
+                        V((N, 16, HID), BF), V((64, HID), F32), V((LE * NCH, CH, FF), BF), V((LE * NCH, FF, CH), BF),
+                        pltpu.SemaphoreType.DMA((LE + 2,)), pltpu.SemaphoreType.DMA((2,))],
         compiler_params=pltpu.CompilerParams(vmem_limit_bytes=67043328),
+        cost_estimate=pl.CostEstimate(flops=4 * LE * CAP * HID * FF, bytes_accessed=64 * 1024 * 1024, transcendentals=0),
         name='weight_grads',
-    )(xl, da, u, dh, y, gx, gg, loss)
+    )(xl, u, dh, da, y, gg, loss)
+
+
+def gradx_kernel(scale, r, one, dlog, gw, g_first, g_now, g_late, gx):
+    tot = r[...].astype(F32) * scale + dot(one[:, :256], g_first[...].reshape(256, CH))
+    tot = tot + dot(dlog[...], gw[...])
+
+    @pl.when(pl.program_id(0) < NOW)
+    def _():
+        gx[...] = (tot + dot(one[:, 256:], g_now[...].reshape(256, CH))).astype(BF)
+
+    @pl.when(pl.program_id(0) >= NOW)
+    def _():
+        gx[...] = (tot + dot(one[:, 256:], g_late[...].reshape(256, CH))).astype(BF)
+
+
+def gradx_call(r, one, dlog, gw, now, later, scale):
+    whole = lambda c: (0, 0)
+    return pl.pallas_call(
+        functools.partial(gradx_kernel, scale),
+        grid=(NCH,),
+        in_specs=[pl.BlockSpec((TOK, CH), lambda c: (0, c)), pl.BlockSpec((TOK, 512), whole), pl.BlockSpec((TOK, 64), whole),
+                  pl.BlockSpec((64, CH), lambda c: (0, c)),
+                  pl.BlockSpec((N, 16, CH), lambda c: (0, 0, c)),
+                  pl.BlockSpec((N, 16, CH), lambda c: (0, 0, jnp.minimum(c, NOW - 1))),
+                  pl.BlockSpec((N, 16, CH), lambda c: (0, 0, NCH + jnp.maximum(c - NOW, 0)))],
+        out_specs=pl.BlockSpec((TOK, CH), lambda c: (0, c)),
+        out_shape=jax.ShapeDtypeStruct((TOK, HID), BF),
+        name='grad_x',
+    )(r, one, dlog, gw, later, now, later)
 
 
 def solution(mesh):
     def device_step(x, gate_w, up_w, down_w, expert_picks, loss_w):
         scale = 1.0 / math.sqrt(TOK * N * HID)
-        y, gx, gg, loss, xl, u, dh, da = comm_call(expert_picks, x, gate_w.T, up_w, down_w, loss_w, scale)
-        grad_up, grad_down, y, gx, gg, loss = wgrad_call(xl, u, dh, da, y, gx, gg, loss)
-        return y.reshape(TOK, HID), loss[0, 0], gx.reshape(TOK, HID), grad_up, grad_down, gg.T
+        gate_t = gate_w.T
+        y, now, later, one, dlog, gg, loss, xl, u, dh, da = comm_call(expert_picks, x, gate_t, up_w, down_w, loss_w, scale)
+        later = lax.all_to_all(later, 'ep', 0, 0, tiled=True)
+        grad_up, grad_down, y, gg, loss = wgrad_call(xl, u, dh, da, y, gg, loss)
+        grad_x = gradx_call(loss_w, one, dlog, gate_t, now, later, scale)
+        return y.reshape(TOK, HID), loss[0, 0], grad_x, grad_up, grad_down, gg.T
 
     return jax.shard_map(device_step, mesh=mesh,
                          in_specs=(P('ep'), P(), P('ep'), P('ep'), P('ep'), P('ep')),

time: 124 us -> 110 us (0.89)
  Pallas kernels: 122 us -> 103 us
  starting transfers between devices: 0 us -> 3.15 us
  waiting for transfers between devices: 0 us -> 2.68 us
    pallas_call x1, Pallas kernels: 97.8 us -> 78.5 us  [comm_call(): pl.pallas_call(functools.partial(comm_kernel, scale), out_shape=[shape((N...]
    all_to_all x0 -> x1, starting transfers between devices: none -> 3.15 us  [device_step(): later = lax.all_to_all(later, 'ep', 0, 0, tiled=True)]
    all_to_all x0 -> x1, waiting for transfers between devices: none -> 2.68 us  [device_step(): later = lax.all_to_all(later, 'ep', 0, 0, tiled=True)]
    pallas_call x1 -> x2, Pallas kernels: 24.6 us -> 24.5 us  [the longest x1 19.4 us: wgrad_call(): pl.pallas_call(wgrad_kernel, in_specs=[any_] * 6 + [smem], out_specs=[any...]
  transfers between devices with their start and end apart: 0 -> 1, of which waited for: 0 -> 1; matrix products, arithmetic and copies ran while one was open for 0% -> 0% of each run, Pallas kernels for 0% -> 18%
where the time goes in v1:
time: 110 us; the launch traced here: 109 us
  Pallas kernels  103 us (94%)
  starting transfers between devices  3.15 us (3%)
  waiting for transfers between devices  2.68 us (2%)
    pallas_call x1, Pallas kernels, comm_call(): pl.pallas_call(functools.partial(comm_kernel, scale), out_shape=[shape((N...  78.5 us
    pallas_call x1, Pallas kernels, wgrad_call(): pl.pallas_call(wgrad_kernel, in_specs=[any_] * 6 + [smem], out_specs=[any...  19.4 us
    pallas_call x1, Pallas kernels, gradx_call(): pl.pallas_call(functools.partial(gradx_kernel, scale), grid=(NCH,), in_sp...  5.05 us
    all_to_all x1, starting transfers between devices, device_step(): later = lax.all_to_all(later, 'ep', 0, 0, tiled=True)  3.15 us
    all_to_all x1, waiting for transfers between devices, device_step(): later = lax.all_to_all(later, 'ep', 0, 0, tiled=True)  2.68 us
  transfers between devices with their start and end apart: 1, of which 1 were waited for; matrix products, arithmetic and copies ran while one was open for 0% of the time, Pallas kernels for 18%

profile of v1, /device:TPU:0, one launch (start us, length us, event | category | flops | bytes accessed | tf_op | source)
XLA Modules:
  0.0 109.5 jit_solution(8770402730078869687)
XLA Ops:
  0.6 78.5 %exchange.1 = (bf16[16,16,2048]{2,1,0:T(8,128)(2,1)}, bf16[16,16,1024]{2,1,0:T(8,128)(2,1)}, bf16[16,16,3072]{2,1,0:T(8,128)(2,1)}, bf16[256,512]{1,0:T(8,128)(2...) custom-call(s32[4,128]{1,0:T(4,128)} %sel_ref.1, ...), custom_call_target="tpu_custom_call" | custom-call | tf_op jit(solution)/shard_map/exchange/pallas_call | solution.py:382
  79.2 3.2 %all-to-all-start = ((bf16[16,16,3072]{2,1,0:T(8,128)(2,1)}), bf16[16,16,3072]{2,1,0:T(8,128)(2,1)}, u32[]{:S(2)}, u32[]{:S(2)}) async-start(bf16[16,16,3072]{2,1,0:T(8,128)(2,1)} %get-tuple-element.33), calls=%async_computation | async-start | bytes 3145728 | tf_op jit(solution)/shard_map/all_to_all | solution.py:511
  82.3 19.4 %weight_grads.1 = (bf16[4,2048,1408]{2,1,0:T(8,128)(2,1)}, bf16[4,1408,2048]{2,1,0:T(8,128)(2,1)}, bf16[16,16,2048]{2,1,0:T(8,128)(2,1)}, f32[64,2048]{1,0:T(8,128)}, f32[1,1]{1,0:T(1,128)}) custom-call(bf16[4,128,2048]{2,1,0:T(8,128)(2,1)} %get-tuple-element.22.xl_in, bf16[4,128,1408]{2,1,0:T(8,128)(2,1)} %get-tuple-element.23.u_in, ...), custom_call_target="tpu_custom_call" | custom-call | flops 5905580032 | bytes 67108864 | tf_op jit(solution)/shard_map/weight_grads/pallas_call | solution.py:463
  101.7 2.7 %all-to-all-done.g_first.g_late = bf16[16,16,3072]{2,1,0:T(8,128)(2,1)} async-done(((bf16[16,16,3072]{2,1,0:T(8,128)(2,1)}), bf16[16,16,3072]{2,1,0:T(8,128)(2,1)}, u32[]{:S(2)}, u32[]{:S(2)}) %all-to-all-start) | async-done | bytes 1572896 | tf_op jit(solution)/shard_map/all_to_all | solution.py:511
  104.4 5.0 %grad_x.1 = bf16[256,2048]{1,0:T(8,128)(2,1)} custom-call(bf16[256,2048]{1,0:T(8,128)(2,1)} %r.1, bf16[256,512]{1,0:T(8,128)(2,1)} %get-tuple-element.31.one, bf16[256,64]{1,0:T(8,128)(2,1)} %get-tuple-element.32.dlog, bf16[64,2048]{1,0:T(8,128)(2,1)} %bitcast.5, bf16[16,16,3072]{2,1,0:T(8,128)(2,1)} %all-to-all-done.g_first.g_late, ...), custom_call_target="tpu_custom_call" | custom-call | tf_op jit(solution)/shard_map/grad_x/pallas_call | solution.py:492
Async XLA Ops:
  79.2 25.2 %all-to-all-start = ((bf16[16,16,3072]{2,1,0:T(8,128)(2,1)}), bf16[16,16,3072]{2,1,0:T(8,128)(2,1)}, u32[]{:S(2)}, u32[]{:S(2)}) async-start(bf16[16,16,3072]{2,1,0:T(8,128)(2,1)} %get-tuple-element.33), calls=%async_computation | async-start | bytes 3145728 | tf_op jit(solution)/shard_map/all_to_all | solution.py:511

commit v2 on v1

--- a/solution.py
+++ b/solution.py
@@ -18,7 +18,8 @@
 FF = 1408
 CH = 512
 NCH = HID // CH
-NOW = 2
+FIRST = 3
+NOW = 4
 ORDER = (14, 15, 6, 10, 12, 7, 11, 13, 2, 4, 8, 3, 5, 9, 1)
 
 
@@ -224,8 +225,8 @@
     def send_now(c):
         cols = pl.ds(c * CH, CH)
         for p in peers:
-            push(gsend.at[1, p, :, cols], gnow_out.at[me, :, cols], p, 6 + c).start()
-        pltpu.make_async_copy(gsend.at[1, me, :, cols], gnow_out.at[me, :, cols], out_sem.at[7 + c]).start()
+            push(gsend.at[1, p, :, cols], gnow_out.at[me, :, cols], p, 13 + c).start()
+        pltpu.make_async_copy(gsend.at[1, me, :, cols], gnow_out.at[me, :, cols], out_sem.at[12 + c]).start()
 
     def bwd(q, carry):
         for j in range(2):
@@ -271,9 +272,10 @@
             send_now(0)
         return carry
     lax.fori_loop(0, 2, bwd, 0)
-    later = [pltpu.make_async_copy(gsend.at[0], glater_out.at[:, :, pl.ds(0, HID)], out_sem.at[5]),
-             pltpu.make_async_copy(gsend.at[1, :, :, pl.ds(NOW * CH, HID - NOW * CH)],
-                                   glater_out.at[:, :, pl.ds(HID, HID - NOW * CH)], out_sem.at[9])]
+    later = [pltpu.make_async_copy(gsend.at[0], glater_out.at[:, :, pl.ds(0, HID)], out_sem.at[5])]
+    if NOW < NCH:
+        later.append(pltpu.make_async_copy(gsend.at[1, :, :, pl.ds(NOW * CH, HID - NOW * CH)],
+                                           glater_out.at[:, :, pl.ds(HID, HID - NOW * CH)], out_sem.at[9]))
     for cp in later:
         cp.start()
     pltpu.make_async_copy(dh_v, dh_out, out_sem.at[2]).start()
@@ -332,6 +334,8 @@
     ggall[core, pl.ds(chip, 1)] = total.reshape(1, 64, 128)
     for p in others:
         push(ggall.at[core, chip], ggall.at[core, chip], p, 11).start()
+    for c in range(2, NOW):
+        send_now(c)
     wait_recv(lossall, 9)
     loss_out[0, 0] = jnp.sum(lossall[...]) * scale
     wait_recv(ggall.at[core], 11, 7)
@@ -344,7 +348,7 @@
     for c in range(NOW):
         cols = pl.ds(c * CH, CH)
         part = gnow_out.at[pl.ds(0, N - 1), :, cols]
-        pltpu.make_async_copy(part, part, recv_sem.at[6 + c]).wait()
+        pltpu.make_async_copy(part, part, recv_sem.at[13 + c]).wait()
 
     wait_send(selall, 0)
     wait_send(gates_all, 2)
@@ -353,8 +357,8 @@
     for c in range(NOW):
         cols = pl.ds(c * CH, CH)
         part = gsend.at[1, pl.ds(0, N - 1), :, cols]
-        pltpu.make_async_copy(part, part, send_sem.at[6 + c]).wait()
-        pltpu.make_async_copy(gsend.at[1, me, :, cols], gnow_out.at[me, :, cols], out_sem.at[7 + c]).wait()
+        pltpu.make_async_copy(part, part, send_sem.at[13 + c]).wait()
+        pltpu.make_async_copy(gsend.at[1, me, :, cols], gnow_out.at[me, :, cols], out_sem.at[12 + c]).wait()
     wait_send(rsend, 3)
     wait_send(lossall, 9)
     push(ggpart.at[1 - core], ggpair, twin, 8).wait_send()
@@ -396,49 +400,66 @@
             V((8, CAP), jnp.int32), V((N, 8, CAP), jnp.int32), V((1, 512), F32), V((N, 1, 512), F32),
             V((1, CH), F32), V((N, 1, CH), F32),
             V((TOK, 512), BF), V((3, TOK, 512), BF), V((LE, CAP, TOK), BF), V((TOK, 64), F32), V((TOK, 64), BF),
-            pltpu.SemaphoreType.DMA((3,)), pltpu.SemaphoreType.DMA((2, 3)), pltpu.SemaphoreType.DMA((12,)),
-            pltpu.SemaphoreType.DMA((13,)), pltpu.SemaphoreType.DMA((13,)),
+            pltpu.SemaphoreType.DMA((3,)), pltpu.SemaphoreType.DMA((2, 3)), pltpu.SemaphoreType.DMA((16,)),
+            pltpu.SemaphoreType.DMA((17,)), pltpu.SemaphoreType.DMA((17,)),
         ],
         compiler_params=pltpu.CompilerParams(collective_id=0, has_side_effects=True, vmem_limit_bytes=67043328),
         name='exchange',
     )(sel, x, gw, up, dn, r)
 
 
-def wgrad_kernel(xl_in, u_in, dh_in, da_in, y_in, gg_in, loss_in, g1, g2, y, gg, loss,
-                 xl_v, u_v, dh_v, da_v, y_v, gg_v, t1, t2, in_sem, out_sem):
+def tile_tools(ins, bufs, outs, tiles, in_sem, out_sem, first):
     def loads(e):
-        return [pltpu.make_async_copy(src.at[e], dst.at[e], in_sem.at[e])
-                for src, dst in ((xl_in, xl_v), (da_in, da_v), (u_in, u_v), (dh_in, dh_v))]
+        return [pltpu.make_async_copy(src.at[e], dst.at[e - first], in_sem.at[e - first]) for src, dst in zip(ins, bufs)]
 
     def stores(i):
         e, c = i // NCH, i % NCH
         cols = pl.ds(pl.multiple_of(c * CH, CH), CH)
-        return [pltpu.make_async_copy(t1.at[i], g1.at[e, cols, :], out_sem.at[0]),
-                pltpu.make_async_copy(t2.at[i], g2.at[e, :, cols], out_sem.at[1])]
-
-    for e in range(LE):
-        for cp in loads(e):
-            cp.start()
-    cp_y = pltpu.make_async_copy(y_in, y_v, in_sem.at[LE])
-    cp_gg = pltpu.make_async_copy(gg_in, gg_v, in_sem.at[LE + 1])
-    cp_y.start()
-    cp_gg.start()
-    loss[0, 0] = loss_in[0, 0]
+        return [pltpu.make_async_copy(tiles[0].at[i - first * NCH], outs[0].at[e, cols, :], out_sem.at[0]),
+                pltpu.make_async_copy(tiles[1].at[i - first * NCH], outs[1].at[e, :, cols], out_sem.at[1])]
 
     def step(i, carry):
         e, c = i // NCH, i % NCH
-
-        @pl.when(c == 0)
-        def _():
-            for cp in loads(e):
-                cp.wait()
+        xl_v, da_v, u_v, dh_v = bufs
         cols = pl.ds(pl.multiple_of(c * CH, CH), CH)
-        t1[i] = dot(xl_v[e, :, cols], da_v[e], 0, 0).astype(BF)
-        t2[i] = dot(u_v[e], dh_v[e, :, cols], 0, 0).astype(BF)
+        tiles[0][i - first * NCH] = dot(xl_v[e - first, :, cols], da_v[e - first], 0, 0).astype(BF)
+        tiles[1][i - first * NCH] = dot(u_v[e - first], dh_v[e - first, :, cols], 0, 0).astype(BF)
         for cp in stores(i):
             cp.start()
         return carry
-    lax.fori_loop(0, LE * NCH, step, 0)
+
+    def finish(i, carry):
+        for cp in stores(i):
+            cp.wait()
+        return carry
+    return loads, step, finish
+
+
+def wgrad1_kernel(xl_in, da_in, u_in, dh_in, y_in, gg_in, loss_in, g1, g2, y, gg, loss,
+                  xl_v, da_v, u_v, dh_v, y_v, gg_v, t1, t2, in_sem, out_sem):
+    loads, step, finish = tile_tools((xl_in, da_in, u_in, dh_in), (xl_v, da_v, u_v, dh_v), (g1, g2), (t1, t2), in_sem, out_sem, 0)
+    cp_y = pltpu.make_async_copy(y_in, y_v, in_sem.at[LE])
+    cp_gg = pltpu.make_async_copy(gg_in, gg_v, in_sem.at[LE + 1])
+    for cp in loads(0):
+        cp.start()
+    loss[0, 0] = loss_in[0, 0]
+
+    def expert(e, carry):
+        for cp in loads(e):
+            cp.wait()
+
+        @pl.when(e + 1 < FIRST)
+        def _():
+            for cp in loads(e + 1):
+                cp.start()
+
+        @pl.when(e == 0)
+        def _():
+            cp_y.start()
+            cp_gg.start()
+        lax.fori_loop(e * NCH, (e + 1) * NCH, step, 0)
+        return carry
+    lax.fori_loop(0, FIRST, expert, 0)
     cp_y.wait()
     cp_gg.wait()
     out_y = pltpu.make_async_copy(y_v, y, in_sem.at[LE])
@@ -447,60 +468,79 @@
     out_gg.start()
     out_y.wait()
     out_gg.wait()
-
-    def finish(i, carry):
-        for cp in stores(i):
-            cp.wait()
-        return carry
-    lax.fori_loop(0, LE * NCH, finish, 0)
-
-
-def wgrad_call(xl, u, dh, da, y, gg, loss):
+    lax.fori_loop(0, FIRST * NCH, finish, 0)
+
+
+def wgrad1_call(xl, da, u, dh, y, gg, loss):
     shape = jax.ShapeDtypeStruct
     any_ = pl.BlockSpec(memory_space=pl.ANY)
     smem = pl.BlockSpec(memory_space=pltpu.SMEM)
     V = pltpu.VMEM
     return pl.pallas_call(
-        wgrad_kernel,
+        wgrad1_kernel,
         in_specs=[any_] * 6 + [smem],
         out_specs=[any_] * 4 + [smem],
         out_shape=[shape((LE, HID, FF), BF), shape((LE, FF, HID), BF), shape((N, 16, HID), BF), shape((64, HID), F32), shape((1, 1), F32)],
-        scratch_shapes=[V((LE, CAP, HID), BF), V((LE, CAP, FF), BF), V((LE, CAP, HID), BF), V((LE, CAP, FF), BF),
-                        V((N, 16, HID), BF), V((64, HID), F32), V((LE * NCH, CH, FF), BF), V((LE * NCH, FF, CH), BF),
+        scratch_shapes=[V((FIRST, CAP, HID), BF), V((FIRST, CAP, FF), BF), V((FIRST, CAP, FF), BF), V((FIRST, CAP, HID), BF),
+                        V((N, 16, HID), BF), V((64, HID), F32), V((FIRST * NCH, CH, FF), BF), V((FIRST * NCH, FF, CH), BF),
                         pltpu.SemaphoreType.DMA((LE + 2,)), pltpu.SemaphoreType.DMA((2,))],
         compiler_params=pltpu.CompilerParams(vmem_limit_bytes=67043328),
-        cost_estimate=pl.CostEstimate(flops=4 * LE * CAP * HID * FF, bytes_accessed=64 * 1024 * 1024, transcendentals=0),
-        name='weight_grads',
-    )(xl, u, dh, da, y, gg, loss)
-
-
-def gradx_kernel(scale, r, one, dlog, gw, g_first, g_now, g_late, gx):
-    tot = r[...].astype(F32) * scale + dot(one[:, :256], g_first[...].reshape(256, CH))
-    tot = tot + dot(dlog[...], gw[...])
-
-    @pl.when(pl.program_id(0) < NOW)
-    def _():
-        gx[...] = (tot + dot(one[:, 256:], g_now[...].reshape(256, CH))).astype(BF)
-
-    @pl.when(pl.program_id(0) >= NOW)
-    def _():
-        gx[...] = (tot + dot(one[:, 256:], g_late[...].reshape(256, CH))).astype(BF)
-
-
-def gradx_call(r, one, dlog, gw, now, later, scale):
-    whole = lambda c: (0, 0)
+        cost_estimate=pl.CostEstimate(flops=FIRST * 4 * CAP * HID * FF, bytes_accessed=48 * 1024 * 1024, transcendentals=0),
+        name='weight_grads_a',
+    )(xl, da, u, dh, y, gg, loss)
+
+
+def wgrad2_kernel(scale, g1_in, g2_in, xl_in, da_in, u_in, dh_in, r_in, one_in, dlog_in, gw_in, now_in, late_in, g1, g2, gx,
+                  xl_v, da_v, u_v, dh_v, r_v, one_v, dlog_v, gw_v, now_v, late_v, gx_v, t1, t2, in_sem, out_sem):
+    rest = LE - FIRST
+    loads, step, finish = tile_tools((xl_in, da_in, u_in, dh_in), (xl_v, da_v, u_v, dh_v), (g1, g2), (t1, t2), in_sem, out_sem, FIRST)
+    for cp in loads(FIRST):
+        cp.start()
+    small = [pltpu.make_async_copy(src, dst, in_sem.at[rest]) for src, dst in
+             ((r_in, r_v), (one_in, one_v), (dlog_in, dlog_v), (gw_in, gw_v), (now_in, now_v), (late_in, late_v))]
+    for cp in small:
+        cp.start()
+    for e in range(FIRST, LE):
+        for cp in loads(e):
+            cp.wait()
+        if e + 1 < LE:
+            for cp in loads(e + 1):
+                cp.start()
+        lax.fori_loop(e * NCH, (e + 1) * NCH, step, 0)
+        if e == FIRST:
+            for cp in small:
+                cp.wait()
+
+            def gstep(c, carry):
+                cols = pl.ds(pl.multiple_of(c * CH, CH), CH)
+                tot = r_v[:, cols].astype(F32) * scale + dot(one_v[:, 0:256], late_v[:, :, cols].reshape(256, CH))
+                tot = tot + dot(one_v[:, 256:512], now_v[:, :, cols].reshape(256, CH))
+                gx_v[:, cols] = (tot + dot(dlog_v[...], gw_v[:, cols])).astype(BF)
+                return carry
+            lax.fori_loop(0, NCH, gstep, 0)
+            pltpu.make_async_copy(gx_v, gx, in_sem.at[rest]).start()
+    pltpu.make_async_copy(gx_v, gx, in_sem.at[rest]).wait()
+    lax.fori_loop(FIRST * NCH, LE * NCH, finish, 0)
+
+
+def wgrad2_call(g1, g2, xl, da, u, dh, r, one, dlog, gw, now, late, scale):
+    shape = jax.ShapeDtypeStruct
+    any_ = pl.BlockSpec(memory_space=pl.ANY)
+    V = pltpu.VMEM
+    rest = LE - FIRST
     return pl.pallas_call(
-        functools.partial(gradx_kernel, scale),
-        grid=(NCH,),
-        in_specs=[pl.BlockSpec((TOK, CH), lambda c: (0, c)), pl.BlockSpec((TOK, 512), whole), pl.BlockSpec((TOK, 64), whole),
-                  pl.BlockSpec((64, CH), lambda c: (0, c)),
-                  pl.BlockSpec((N, 16, CH), lambda c: (0, 0, c)),
-                  pl.BlockSpec((N, 16, CH), lambda c: (0, 0, jnp.minimum(c, NOW - 1))),
-                  pl.BlockSpec((N, 16, CH), lambda c: (0, 0, NCH + jnp.maximum(c - NOW, 0)))],
-        out_specs=pl.BlockSpec((TOK, CH), lambda c: (0, c)),
-        out_shape=jax.ShapeDtypeStruct((TOK, HID), BF),
-        name='grad_x',
-    )(r, one, dlog, gw, later, now, later)
+        functools.partial(wgrad2_kernel, scale),
+        in_specs=[any_] * 12,
+        out_specs=[any_] * 3,
+        out_shape=[shape((LE, HID, FF), BF), shape((LE, FF, HID), BF), shape((TOK, HID), BF)],
+        scratch_shapes=[V((rest, CAP, HID), BF), V((rest, CAP, FF), BF), V((rest, CAP, FF), BF), V((rest, CAP, HID), BF),
+                        V((TOK, HID), BF), V((TOK, 512), BF), V((TOK, 64), BF), V((64, HID), BF), V((N, 16, HID), BF), V((N, 16, HID), BF),
+                        V((TOK, HID), BF), V((rest * NCH, CH, FF), BF), V((rest * NCH, FF, CH), BF),
+                        pltpu.SemaphoreType.DMA((rest + 1,)), pltpu.SemaphoreType.DMA((2,))],
+        input_output_aliases={0: 0, 1: 1},
+        compiler_params=pltpu.CompilerParams(vmem_limit_bytes=67043328),
+        name='weight_grads_b',
+    )(g1, g2, xl, da, u, dh, r, one, dlog, gw, now, late)
 
 
 def solution(mesh):
@@ -509,8 +549,8 @@
         gate_t = gate_w.T
         y, now, later, one, dlog, gg, loss, xl, u, dh, da = comm_call(expert_picks, x, gate_t, up_w, down_w, loss_w, scale)
         later = lax.all_to_all(later, 'ep', 0, 0, tiled=True)
-        grad_up, grad_down, y, gg, loss = wgrad_call(xl, u, dh, da, y, gg, loss)
-        grad_x = gradx_call(loss_w, one, dlog, gate_t, now, later, scale)
+        grad_up, grad_down, y, gg, loss = wgrad1_call(xl, da, u, dh, y, gg, loss)
+        grad_up, grad_down, grad_x = wgrad2_call(grad_up, grad_down, xl, da, u, dh, loss_w, one, dlog, gate_t, now, later, scale)
         return y.reshape(TOK, HID), loss[0, 0], grad_x, grad_up, grad_down, gg.T
 
     return jax.shard_map(device_step, mesh=mesh,

time: 110 us -> 109 us (level)
  waiting for transfers between devices: 2.68 us -> 0.38 us
  Pallas kernels: 103 us -> 105 us
    pallas_call x1, Pallas kernels: 78.5 us -> 81.8 us  [comm_call(): pl.pallas_call(functools.partial(comm_kernel, scale), out_shape=[shape((N...]
    all_to_all x1, waiting for transfers between devices: 2.68 us -> 0.38 us  [device_step(): later = lax.all_to_all(later, 'ep', 0, 0, tiled=True)]
    pallas_call x2, Pallas kernels: 24.5 us -> 23.2 us  [the longest x1 15.5 us: wgrad1_call(): pl.pallas_call(wgrad1_kernel, in_specs=[any_] * 6 + [smem], out_specs=[an...]
  transfers between devices with their start and end apart: 1 -> 1, of which waited for: 1 -> 1; matrix products, arithmetic and copies ran while one was open for 0% -> 0% of each run, Pallas kernels for 18% -> 14%
where the time goes in v2:
time: 109 us
  Pallas kernels  105 us (96%)
  starting transfers between devices  3.1 us (3%)
    pallas_call x1, Pallas kernels, comm_call(): pl.pallas_call(functools.partial(comm_kernel, scale), out_shape=[shape((N...  81.8 us
    pallas_call x1, Pallas kernels, wgrad1_call(): pl.pallas_call(wgrad1_kernel, in_specs=[any_] * 6 + [smem], out_specs=[an...  15.5 us
    pallas_call x1, Pallas kernels, wgrad2_call(): pl.pallas_call(functools.partial(wgrad2_kernel, scale), in_specs=[any_] *...  7.69 us
    all_to_all x1, starting transfers between devices, device_step(): later = lax.all_to_all(later, 'ep', 0, 0, tiled=True)  3.1 us
  transfers between devices with their start and end apart: 1, of which 1 were waited for; matrix products, arithmetic and copies ran while one was open for 0% of the time, Pallas kernels for 14%

profile of v2, /device:TPU:0, one launch (start us, length us, event | category | flops | bytes accessed | tf_op | source)
XLA Modules:
  0.0 109.2 jit_solution(3235700652371904438)
XLA Ops:
  0.6 81.8 %exchange.1 = (bf16[16,16,2048]{2,1,0:T(8,128)(2,1)}, bf16[16,16,2048]{2,1,0:T(8,128)(2,1)}, bf16[16,16,2048]{2,1,0:T(8,128)(2,1)}, bf16[256,512]{1,0:T(8,128)(2...) custom-call(s32[4,128]{1,0:T(4,128)} %sel_ref.1, ...), custom_call_target="tpu_custom_call" | custom-call | tf_op jit(solution)/shard_map/exchange/pallas_call | solution.py:386
  82.5 3.1 %all-to-all-start = ((bf16[16,16,2048]{2,1,0:T(8,128)(2,1)}), bf16[16,16,2048]{2,1,0:T(8,128)(2,1)}, u32[]{:S(2)}, u32[]{:S(2)}) async-start(bf16[16,16,2048]{2,1,0:T(8,128)(2,1)} %get-tuple-element.39), calls=%async_computation | async-start | bytes 2097152 | tf_op jit(solution)/shard_map/all_to_all | solution.py:551
  85.6 15.5 %weight_grads_a.1 = (bf16[4,2048,1408]{2,1,0:T(8,128)(2,1)}, bf16[4,1408,2048]{2,1,0:T(8,128)(2,1)}, bf16[16,16,2048]{2,1,0:T(8,128)(2,1)}, f32[64,2048]{1,0:T(8,128)}, f32[1,1]{1,0:T(1,128)}) custom-call(bf16[4,128,2048]{2,1,0:T(8,128)(2,1)} %get-tuple-element.25.xl_in, bf16[4,128,1408]{2,1,0:T(8,128)(2,1)} %get-tuple-element.26.da_in, ...), custom_call_target="tpu_custom_call" | custom-call | flops 4429185024 | bytes 50331648 | tf_op jit(solution)/shard_map/weight_grads_a/pallas_call | solution.py:479
  101.1 0.4 all-to-all-done.late_in
  101.5 7.7 %weight_grads_b.1 = (bf16[4,2048,1408]{2,1,0:T(8,128)(2,1)}, bf16[4,1408,2048]{2,1,0:T(8,128)(2,1)}, bf16[256,2048]{1,0:T(8,128)(2,1)}) custom-call(bf16[4,2048,1408]{2,1,0:T(8,128)(2,1)} %get-tuple-element.34.g1_in, bf16[4,1408,2048]{2,1,0:T(8,128)(2,1)} %get-tuple-element.35.g2_in, ...), custom_call_target="tpu_custom_call", output_to_operand_aliasing={{0}: (0, {}), {1}: (1, {})} | custom-call | tf_op jit(solution)/shard_map/weight_grads_b/pallas_call | solution.py:531
Async XLA Ops:
  82.5 19.0 %all-to-all-start = ((bf16[16,16,2048]{2,1,0:T(8,128)(2,1)}), bf16[16,16,2048]{2,1,0:T(8,128)(2,1)}, u32[]{:S(2)}, u32[]{:S(2)}) async-start(bf16[16,16,2048]{2,1,0:T(8,128)(2,1)} %get-tuple-element.39), calls=%async_computation | async-start | bytes 2097152 | tf_op jit(solution)/shard_map/all_to_all | solution.py:551
